TPU v7x, 32 devices: a whole 2x2x4 slice. The times are simulated.
32 devices in a mesh: expert: 4 (over z), shard: 8 (over y, x, core).
Axes of the slice: x: 2, y: 2, z: 4, core: 2. Of those that a mesh axis runs over, the one named last changes fastest.
Arguments:
- master_down: float32 [16, 6400, 4096], P('expert', None, 'shard'), may hold values from -0.109375 to 0.109375
- second_down: bfloat16 [16, 6400, 4096], P('expert', None, 'shard'), may hold values from -0.0390625 to 0.0390625
- router_weight: float32 [4096, 16], P('shard', 'expert'), may hold values from -0.09375 to 0.09375
- router_gain: float32 [4096], P('shard'), may hold values from 0.25 to 1.75
Outputs:
- final_down: bfloat16 [16, 6400, 4096], P('expert', 'shard')
- scale_down: float32 [16, 6400], P('expert', 'shard')
- serve_router: bfloat16 [4096, 16], replicated
All inputs are finite; a program needn't handle non-finite values.
Results may differ from a plain program's by a relative error of at most 0.001.
Values may be sent and summed in bfloat16 or wider, within the bound.
A program may use at most 256 MiB of HBM per device.

v0:
```python
import jax
import jax.numpy as jnp
from jax import lax
from jax.sharding import PartitionSpec as P


def local(master_down, second_down, router_weight, router_gain):
    merged_down = master_down + second_down.astype(jnp.float32)
    total_down = lax.psum(jnp.sum(merged_down * merged_down, axis=2), "shard")
    scale_down = jnp.sqrt(total_down)
    narrow_down = (merged_down / jnp.expand_dims(scale_down, 2)).astype(jnp.bfloat16)
    final_down = lax.all_to_all(narrow_down, "shard", split_axis=1, concat_axis=2, tiled=True)
    scale_down = lax.dynamic_slice_in_dim(
        scale_down, lax.axis_index("shard") * final_down.shape[1], final_down.shape[1], axis=1
    )
    part_router = (router_weight * router_gain[:, None]).astype(jnp.bfloat16)
    row_router = lax.all_gather(part_router, "shard", axis=0, tiled=True)
    serve_router = lax.all_gather(row_router, "expert", axis=1, tiled=True)
    return (final_down, scale_down, serve_router)


def solution(mesh):
    return jax.shard_map(
        local,
        mesh=mesh,
        in_specs=(
            P("expert", None, "shard"),
            P("expert", None, "shard"),
            P("shard", "expert"),
            P("shard"),
        ),
        out_specs=(P("expert", "shard", None), P("expert", "shard"), P()),
        check_vma=False,
    )
```

profile of v0, /device:TPU:0, one launch (start us, length us, event | category | flops | bytes accessed | tf_op | source)
XLA Modules:
  0.0 554.8 jit_solution(7517493062815123618)
XLA Ops:
  7.2 0.0 all-reduce.2.cloned.1.call-start
  7.2 24.2 %multiply_reduce_fusion = f32[4,6400]{1,0:T(4,128)S(1)} fusion(f32[4,6400,512]{2,1,0:T(8,128)} %param.4, bf16[4,6400,512]{2,1,0:T(8,128)(2,1)} %param.5), kind=kLoop, calls=%fused_computation.1 | loop fusion | flops 52403200 | bytes 78745600 | tf_op jit(solution)/shard_map/reduce_sum | solution.py:9
  31.4 2.3 copy.21
  33.7 0.0 all-reduce.2.cloned.1.call-update
  33.7 73.6 %all-reduce.2.cloned.1.call-done = f32[4,6400]{0,1:T(8,128)} async-done(((f32[4,6400]{0,1:T(8,128)}), f32[4,6400]{0,1:T(8,128)}) %all-reduce.2.cloned.1.call-update) | async-done | bytes 102416 | tf_op jit(solution)/shard_map/psum | solution.py:9
  107.3 2.7 sqrt.3
  110.0 1.2 copy.17
  111.3 34.3 %divide_convert_fusion = bf16[4,6400,512]{2,1,0:T(8,128)(2,1)} fusion(f32[4,6400,512]{2,1,0:T(8,128)} %param.4, bf16[4,6400,512]{2,1,0:T(8,128)(2,1)} %param.5, f32[4,6400]{1,0:T(4,128)S(1)} %copy.17), kind=kLoop, calls=%fused_computation | loop fusion | flops 52428800 | bytes 104960000 | tf_op jit(solution)/shard_map/convert_element_type | solution.py:11
  145.5 33.4 %copy.18 = bf16[4,6400,512]{2,0,1:T(4,128)(2,1)} copy(bf16[4,6400,512]{2,1,0:T(8,128)(2,1)} %divide_convert_fusion) | data formatting | bytes 52428800 | tf_op jit(solution)/shard_map/convert_element_type | solution.py:11
  178.9 0.0 copy-start
  178.9 0.0 copy-start.1
  178.9 6.6 %all-to-all-start = ((bf16[4,6400,512]{2,0,1:T(4,128)(2,1)}), bf16[4,6400,512]{2,0,1:T(4,128)(2,1)}, u32[]{:S(2)}, u32[]{:S(2)}) async-start(bf16[4,6400,512]{2,0,1:T(4,128)(2,1)} %copy.18), calls=%async_computation | async-start | bytes 52428800 | tf_op jit(solution)/shard_map/all_to_all | solution.py:12
  185.6 0.0 copy-done
  185.6 0.0 copy-done.1
  185.6 288.2 %all_gather.6 = bf16[4096,4]{0,1:T(4,128)(2,1)S(1)} all-gather(bf16[512,4]{0,1:T(4,128)(2,1)S(1)} %multiply_convert_fusion), channel_id=1, replica_groups=mesh['expert'=4,'shard'=8] {'shard'}, dimensions={0}, use_global_device_ids=true | all-gather | bytes 36864 | tf_op jit(solution)/shard_map/all_gather | solution.py:17
  473.8 13.5 %all-gather = bf16[4,4,4096]{2,1,0:T(4,128)(2,1)S(1)} all-gather(bf16[1,4,4096]{2,1,0:T(4,128)(2,1)S(1)} %bitcast.9), channel_id=1, replica_groups=mesh['expert'=4,'shard'=8] {'expert'}, dimensions={0}, use_global_device_ids=true | all-gather | bytes 163840 | tf_op jit(solution)/shard_map/all_gather | solution.py:18
  487.3 0.7 reshape.9
  488.0 0.8 constant_dynamic-slice_fusion
  488.7 1.8 copy.20
  490.5 0.0 all-to-all-done
  490.5 18.2 %copy.19 = bf16[4,800,8,512]{3,2,1,0:T(8,128)(2,1)} copy(bf16[4,800,8,512]{3,0,1,2:T(4,128)(2,1)} %bitcast.1) | data formatting | bytes 52428800 | tf_op jit(solution)/shard_map/all_to_all | solution.py:12
  508.7 39.2 %all_to_all.16 = bf16[4,800,4096]{2,1,0:T(8,128)(2,1)} reshape(bf16[4,800,8,512]{3,2,1,0:T(8,128)(2,1)} %copy.19) | data formatting | bytes 52428800 | tf_op jit(solution)/shard_map/all_to_all | solution.py:12
  (1 shorter events, 0.0 us)
Async XLA Ops:
  7.2 100.2 %all-reduce.2.cloned.1.call-start = ((), (), s32[]{:S(2)}) async-start(), calls=%async_computation.1 | async-start | bytes 6553600 | tf_op jit(solution)/shard_map/psum | solution.py:9
  178.9 6.7 %copy-start = (f32[512,4]{0,1:T(4,128)S(1)}, f32[512,4]{0,1:T(4,128)}, u32[]{:S(2)}) copy-start(f32[512,4]{0,1:T(4,128)} %param.6) | copy-start | bytes 24580
  178.9 6.7 %copy-start.1 = (f32[512]{0:T(512)S(1)}, f32[512]{0:T(512)}, u32[]{:S(2)}) copy-start(f32[512]{0:T(512)} %param.7) | copy-start | bytes 6148
  178.9 311.6 %all-to-all-start = ((bf16[4,6400,512]{2,0,1:T(4,128)(2,1)}), bf16[4,6400,512]{2,0,1:T(4,128)(2,1)}, u32[]{:S(2)}, u32[]{:S(2)}) async-start(bf16[4,6400,512]{2,0,1:T(4,128)(2,1)} %copy.18), calls=%async_computation | async-start | bytes 52428800 | tf_op jit(solution)/shard_map/all_to_all | solution.py:12
Sparse Core Ops, SparseCore 0:
  33.9 73.4 all-reduce.1
where the time goes:
time: 556 us; the launch traced here: 555 us
  blocking collectives  302 us (54%)
  local copies, waits for them, and re-layouts  100 us (18%)
  waiting for transfers between devices  73.6 us (13%)
  other arithmetic  58.5 us (11%)
  between operations  14.1 us (3%)
  starting transfers between devices  6.67 us (1%)
    all_gather x1, blocking collectives, local(): row_router = lax.all_gather(part_router, 'shard', axis=0, tiled=True)  288 us
    psum x1, waiting for transfers between devices, local(): total_down = lax.psum(jnp.sum(merged_down * merged_down, axis=2), 'shard')  73.6 us
    all_to_all x2, local copies, waits for them, and re-layouts, local(): lax.all_to_all(narrow_down, 'shard', split_axis=1, concat_axis=2, tiled=T...  57.4 us
    convert_element_type x1, other arithmetic, local(): (merged_down / jnp.expand_dims(scale_down, 2)).astype(jnp.bfloat16)  34.3 us
    convert_element_type x1, local copies, waits for them, and re-layouts, local(): (merged_down / jnp.expand_dims(scale_down, 2)).astype(jnp.bfloat16)  33.4 us
    reduce_sum x1, other arithmetic, local(): total_down = lax.psum(jnp.sum(merged_down * merged_down, axis=2), 'shard')  24.2 us
    all_gather x1, blocking collectives, local(): serve_router = lax.all_gather(row_router, 'expert', axis=1, tiled=True)  13.5 us
  transfers between devices with their start and end apart: 2, of which 1 were waited for; matrix products, arithmetic and copies ran while one was open for 1% of the time, Pallas kernels for 0%

commit v1 on v0

--- a/solution.py
+++ b/solution.py
@@ -4,9 +4,13 @@
 from jax.sharding import PartitionSpec as P
 
 
+def answer_columns_now(a0):
+    return jnp.sum(lax.all_gather(a0, "shard"), axis=0)
+
+
 def local(master_down, second_down, router_weight, router_gain):
     merged_down = master_down + second_down.astype(jnp.float32)
-    total_down = lax.psum(jnp.sum(merged_down * merged_down, axis=2), "shard")
+    total_down = answer_columns_now(jnp.sum(merged_down * merged_down, axis=2))
     scale_down = jnp.sqrt(total_down)
     narrow_down = (merged_down / jnp.expand_dims(scale_down, 2)).astype(jnp.bfloat16)
     final_down = lax.all_to_all(narrow_down, "shard", split_axis=1, concat_axis=2, tiled=True)

time: 556 us -> 475 us (0.85)
  waiting for transfers between devices: 73.6 us -> 0.01 us
  between operations: 14.1 us -> 0.71 us
  blocking collectives: 302 us -> 314 us
    psum x1 -> x0, waiting for transfers between devices: 73.6 us -> none  [local(): total_down = lax.psum(jnp.sum(merged_down * merged_down, axis=2), 'shard')]
    all_gather x0 -> x1, blocking collectives: none -> 12 us  [answer_columns_now(): return jnp.sum(lax.all_gather(a0, 'shard'), axis=0)]
    reduce_sum x1 -> x2, other arithmetic: 24.2 us -> 24.4 us  [the longest x1 24.2 us: local(): total_down = answer_columns_now(jnp.sum(merged_down * merged_down, axis=2))]
  transfers between devices with their start and end apart: 2 -> 1, of which waited for: 1 -> 0; matrix products, arithmetic and copies ran while one was open for 1% -> 0% of each run, Pallas kernels for 0% -> 0%
where the time goes in v1:
time: 475 us; the launch traced here: 474 us
  blocking collectives  314 us (66%)
  local copies, waits for them, and re-layouts  94.5 us (20%)
  other arithmetic  58.7 us (12%)
  starting transfers between devices  6.5 us (1%)
    all_gather x1, blocking collectives, local(): row_router = lax.all_gather(part_router, 'shard', axis=0, tiled=True)  288 us
    all_to_all x2, local copies, waits for them, and re-layouts, local(): lax.all_to_all(narrow_down, 'shard', split_axis=1, concat_axis=2, tiled=T...  57.4 us
    convert_element_type x1, other arithmetic, local(): (merged_down / jnp.expand_dims(scale_down, 2)).astype(jnp.bfloat16)  34.3 us
    convert_element_type x1, local copies, waits for them, and re-layouts, local(): (merged_down / jnp.expand_dims(scale_down, 2)).astype(jnp.bfloat16)  33.4 us
    reduce_sum x1, other arithmetic, local(): total_down = answer_columns_now(jnp.sum(merged_down * merged_down, axis=2))  24.2 us
    all_gather x1, blocking collectives, local(): serve_router = lax.all_gather(row_router, 'expert', axis=1, tiled=True)  13.6 us
    all_gather x1, blocking collectives, answer_columns_now(): return jnp.sum(lax.all_gather(a0, 'shard'), axis=0)  12 us
  transfers between devices with their start and end apart: 1, of which 0 were waited for; matrix products, arithmetic and copies ran while one was open for 0% of the time, Pallas kernels for 0%

profile of v1, /device:TPU:0, one launch (start us, length us, event | category | flops | bytes accessed | tf_op | source)
XLA Modules:
  0.0 474.2 jit_solution(13347673864453672481)
XLA Ops:
  0.6 24.2 %multiply_reduce_fusion = f32[4,6400]{1,0:T(4,128)S(1)} fusion(f32[4,6400,512]{2,1,0:T(8,128)} %param.4, bf16[4,6400,512]{2,1,0:T(8,128)(2,1)} %param.5), kind=kLoop, calls=%fused_computation.1 | loop fusion | flops 52403200 | bytes 78745600 | tf_op jit(solution)/shard_map/reduce_sum | solution.py:13
  24.9 1.1 copy.21
  26.0 1.2 copy.18
  27.2 12.0 %all-gather.1 = f32[8,4,6400]{2,1,0:T(4,128)S(1)} all-gather(f32[1,4,6400]{2,1,0:T(4,128)S(1)} %copy.18), channel_id=2, replica_groups=mesh['expert'=4,'shard'=8] {'shard'}, dimensions={0}, use_global_device_ids=true | all-gather | bytes 921600 | tf_op jit(solution)/shard_map/all_gather | solution.py:8
  39.2 0.1 reduce_sum.19
  39.4 0.1 sqrt.7
  39.4 34.3 %divide_convert_fusion = bf16[4,6400,512]{2,1,0:T(8,128)(2,1)} fusion(f32[4,6400,512]{2,1,0:T(8,128)} %param.4, bf16[4,6400,512]{2,1,0:T(8,128)(2,1)} %param.5, f32[4,6400]{1,0:T(4,128)S(1)} %sqrt.7), kind=kLoop, calls=%fused_computation | loop fusion | flops 52428800 | bytes 104960000 | tf_op jit(solution)/shard_map/convert_element_type | solution.py:15
  73.7 0.0 copy-start
  73.7 0.0 copy-start.1
  73.7 33.4 %copy.19 = bf16[4,6400,512]{2,0,1:T(4,128)(2,1)} copy(bf16[4,6400,512]{2,1,0:T(8,128)(2,1)} %divide_convert_fusion) | data formatting | bytes 52428800 | tf_op jit(solution)/shard_map/convert_element_type | solution.py:15
  107.1 6.5 %all-to-all-start = ((bf16[4,6400,512]{2,0,1:T(4,128)(2,1)}), bf16[4,6400,512]{2,0,1:T(4,128)(2,1)}, u32[]{:S(2)}, u32[]{:S(2)}) async-start(bf16[4,6400,512]{2,0,1:T(4,128)(2,1)} %copy.19), calls=%async_computation | async-start | bytes 52428800 | tf_op jit(solution)/shard_map/all_to_all | solution.py:16
  113.6 0.0 copy-done
  113.6 0.0 copy-done.1
  113.7 288.2 %all_gather.14 = bf16[4096,4]{0,1:T(4,128)(2,1)S(1)} all-gather(bf16[512,4]{0,1:T(4,128)(2,1)S(1)} %multiply_convert_fusion), channel_id=1, replica_groups=mesh['expert'=4,'shard'=8] {'shard'}, dimensions={0}, use_global_device_ids=true | all-gather | bytes 36864 | tf_op jit(solution)/shard_map/all_gather | solution.py:21
  401.8 13.6 %all-gather.2 = bf16[4,4,4096]{2,1,0:T(4,128)(2,1)S(1)} all-gather(bf16[1,4,4096]{2,1,0:T(4,128)(2,1)S(1)} %bitcast.11), channel_id=1, replica_groups=mesh['expert'=4,'shard'=8] {'expert'}, dimensions={0}, use_global_device_ids=true | all-gather | bytes 163840 | tf_op jit(solution)/shard_map/all_gather | solution.py:22
  415.4 0.7 reshape.14
  416.1 0.7 constant_dynamic-slice_fusion
  416.8 0.0 all-to-all-done
  416.8 18.2 %copy.20 = bf16[4,800,8,512]{3,2,1,0:T(8,128)(2,1)} copy(bf16[4,800,8,512]{3,0,1,2:T(4,128)(2,1)} %bitcast.2) | data formatting | bytes 52428800 | tf_op jit(solution)/shard_map/all_to_all | solution.py:16
  435.0 39.2 %all_to_all.16 = bf16[4,800,4096]{2,1,0:T(8,128)(2,1)} reshape(bf16[4,800,8,512]{3,2,1,0:T(8,128)(2,1)} %copy.20) | data formatting | bytes 52428800 | tf_op jit(solution)/shard_map/all_to_all | solution.py:16
  (1 shorter events, 0.0 us)
Async XLA Ops:
  73.7 39.9 %copy-start = (f32[512,4]{0,1:T(4,128)S(1)}, f32[512,4]{0,1:T(4,128)}, u32[]{:S(2)}) copy-start(f32[512,4]{0,1:T(4,128)} %param.6) | copy-start | bytes 24580
  73.7 39.9 %copy-start.1 = (f32[512]{0:T(512)S(1)}, f32[512]{0:T(512)}, u32[]{:S(2)}) copy-start(f32[512]{0:T(512)} %param.7) | copy-start | bytes 6148
  107.1 309.7 %all-to-all-start = ((bf16[4,6400,512]{2,0,1:T(4,128)(2,1)}), bf16[4,6400,512]{2,0,1:T(4,128)(2,1)}, u32[]{:S(2)}, u32[]{:S(2)}) async-start(bf16[4,6400,512]{2,0,1:T(4,128)(2,1)} %copy.19), calls=%async_computation | async-start | bytes 52428800 | tf_op jit(solution)/shard_map/all_to_all | solution.py:16

commit v2 on v0

--- a/solution.py
+++ b/solution.py
@@ -9,7 +9,13 @@
     total_down = lax.psum(jnp.sum(merged_down * merged_down, axis=2), "shard")
     scale_down = jnp.sqrt(total_down)
     narrow_down = (merged_down / jnp.expand_dims(scale_down, 2)).astype(jnp.bfloat16)
-    final_down = lax.all_to_all(narrow_down, "shard", split_axis=1, concat_axis=2, tiled=True)
+    _deliver_works = lambda piece_in: jnp.concatenate(
+        jax.lax.all_to_all(
+            jnp.stack(jnp.split(piece_in, jax.lax.axis_size("shard"), 1)), "shard", 0, 0
+        ),
+        axis=2,
+    )
+    final_down = _deliver_works(narrow_down)
     scale_down = lax.dynamic_slice_in_dim(
         scale_down, lax.axis_index("shard") * final_down.shape[1], final_down.shape[1], axis=1
     )

time: 556 us -> 488 us (0.88)
  local copies, waits for them, and re-layouts: 100 us -> 50.8 us
  waiting for transfers between devices: 73.6 us -> 54.9 us
    all_to_all x2 -> x0, local copies, waits for them, and re-layouts: 57.4 us -> none  [local(): lax.all_to_all(narrow_down, 'shard', split_axis=1, concat_axis=2, tiled=T...]
    convert_element_type x1 -> x0, local copies, waits for them, and re-layouts: 33.4 us -> none  [local(): (merged_down / jnp.expand_dims(scale_down, 2)).astype(jnp.bfloat16)]
    unnamed x7 -> x12, local copies, waits for them, and re-layouts: 4.75 us -> 27.5 us
    psum x1, waiting for transfers between devices: 73.6 us -> 54.9 us  [local(): total_down = lax.psum(jnp.sum(merged_down * merged_down, axis=2), 'shard')]
    reshape x0 -> x1, local copies, waits for them, and re-layouts: none -> 17.9 us  [local(): jnp.concatenate(jax.lax.all_to_all(jnp.stack(jnp.split(piece_in, jax.lax....]
  transfers between devices with their start and end apart: 2 -> 2, of which waited for: 1 -> 1; matrix products, arithmetic and copies ran while one was open for 1% -> 0% of each run, Pallas kernels for 0% -> 0%
where the time goes in v2:
time: 488 us; the launch traced here: 487 us
  blocking collectives  302 us (62%)
  other arithmetic  59.2 us (12%)
  waiting for transfers between devices  54.9 us (11%)
  local copies, waits for them, and re-layouts  50.8 us (10%)
  between operations  14.1 us (3%)
  starting transfers between devices  6.66 us (1%)
    all_gather x1, blocking collectives, local(): row_router = lax.all_gather(part_router, 'shard', axis=0, tiled=True)  288 us
    psum x1, waiting for transfers between devices, local(): total_down = lax.psum(jnp.sum(merged_down * merged_down, axis=2), 'shard')  54.9 us
    convert_element_type x1, other arithmetic, local(): (merged_down / jnp.expand_dims(scale_down, 2)).astype(jnp.bfloat16)  34.3 us
    unnamed x12, local copies, waits for them, and re-layouts  27.5 us
    reduce_sum x1, other arithmetic, local(): total_down = lax.psum(jnp.sum(merged_down * merged_down, axis=2), 'shard')  24.9 us
    reshape x1, local copies, waits for them, and re-layouts, local(): jnp.concatenate(jax.lax.all_to_all(jnp.stack(jnp.split(piece_in, jax.lax....  17.9 us
    all_gather x1, blocking collectives, local(): serve_router = lax.all_gather(row_router, 'expert', axis=1, tiled=True)  13.5 us
  transfers between devices with their start and end apart: 2, of which 1 were waited for; matrix products, arithmetic and copies ran while one was open for 0% of the time, Pallas kernels for 0%

profile of v2, /device:TPU:0, one launch (start us, length us, event | category | flops | bytes accessed | tf_op | source)
XLA Modules:
  0.0 487.3 jit_solution(10689226386606609922)
XLA Ops:
  7.2 0.0 all-reduce.2.cloned.1.call-start
  7.2 24.9 %multiply_reduce_fusion = f32[4,6400]{1,0:T(4,128)} fusion(f32[4,6400,512]{2,1,0:T(8,128)} %param.4, bf16[4,6400,512]{2,1,0:T(8,128)(2,1)} %param.5), kind=kLoop, calls=%fused_computation.1 | loop fusion | flops 52403200 | bytes 78745600 | tf_op jit(solution)/shard_map/reduce_sum | solution.py:9
  32.1 0.0 all-reduce.2.cloned.1.call-update
  32.1 54.9 %all-reduce.2.cloned.1.call-done = f32[4,6400]{1,0:T(4,128)} async-done(((f32[4,6400]{1,0:T(4,128)}), f32[4,6400]{1,0:T(4,128)}) %all-reduce.2.cloned.1.call-update) | async-done | bytes 102416 | tf_op jit(solution)/shard_map/psum | solution.py:9
  87.0 0.9 sqrt.3
  88.0 34.3 %divide_convert_fusion = bf16[4,6400,512]{2,1,0:T(8,128)(2,1)} fusion(f32[4,6400,512]{2,1,0:T(8,128)} %param.4, bf16[4,6400,512]{2,1,0:T(8,128)(2,1)} %param.5, f32[4,6400]{1,0:T(4,128)S(1)} %sqrt.3), kind=kLoop, calls=%fused_computation | loop fusion | flops 52428800 | bytes 104960000 | tf_op jit(solution)/shard_map/convert_element_type | solution.py:11
  122.2 3.8 fusion.7
  126.1 3.8 fusion.6
  129.9 3.8 fusion.5
  133.7 3.8 fusion.4
  137.6 3.9 fusion.3
  141.4 3.8 fusion.2
  145.2 3.8 fusion.1
  149.1 3.8 fusion
  152.9 0.0 copy-start
  152.9 6.6 %all-to-all-start = ((bf16[8,4,800,512]{3,2,1,0:T(8,128)(2,1)}), bf16[8,4,800,512]{3,2,1,0:T(8,128)(2,1)}, u32[]{:S(2)}, u32[]{:S(2)}) async-start(bf16[8,4,800,512]{3,2,1,0:T(8,128)(2,1)} %fusion), calls=%async_computation | async-start | bytes 52428800 | tf_op jit(solution)/shard_map/all_to_all | solution.py:13
  159.5 0.0 copy-done
  159.5 0.0 copy-done.1
  159.6 288.2 %all_gather.6 = bf16[4096,4]{0,1:T(4,128)(2,1)S(1)} all-gather(bf16[512,4]{0,1:T(4,128)(2,1)S(1)} %multiply_convert_fusion), channel_id=1, replica_groups=mesh['expert'=4,'shard'=8] {'shard'}, dimensions={0}, use_global_device_ids=true | all-gather | bytes 36864 | tf_op jit(solution)/shard_map/all_gather | solution.py:23
  447.7 13.5 %all-gather = bf16[4,4,4096]{2,1,0:T(4,128)(2,1)S(1)} all-gather(bf16[1,4,4096]{2,1,0:T(4,128)(2,1)S(1)} %bitcast.40), channel_id=1, replica_groups=mesh['expert'=4,'shard'=8] {'expert'}, dimensions={0}, use_global_device_ids=true | all-gather | bytes 163840 | tf_op jit(solution)/shard_map/all_gather | solution.py:24
  461.2 0.7 reshape.17
  461.9 0.7 constant_dynamic-slice_fusion
  462.6 0.0 all-to-all-done
  462.6 17.9 %copy.9 = bf16[8,4,100,8,512]{4,3,0,2,1:T(8,128)(2,1)} copy(bf16[8,4,100,8,512]{4,3,2,1,0:T(8,128)(2,1)} %bitcast.13) | data formatting | bytes 52428800 | tf_op jit(solution)/shard_map/reshape | solution.py:12
  (2 shorter events, 0.0 us)
Async XLA Ops:
  7.2 79.8 %all-reduce.2.cloned.1.call-start = ((), (), s32[]{:S(2)}) async-start(), calls=%async_computation.1 | async-start | bytes 204800 | tf_op jit(solution)/shard_map/psum | solution.py:9
  152.9 6.6 %copy-start = (f32[512,4]{0,1:T(4,128)S(1)}, f32[512,4]{0,1:T(4,128)}, u32[]{:S(2)}) copy-start(f32[512,4]{0,1:T(4,128)} %param.6) | copy-start | bytes 24580
  152.9 6.6 %copy-start.1 = (f32[512]{0:T(512)S(1)}, f32[512]{0:T(512)}, u32[]{:S(2)}) copy-start(f32[512]{0:T(512)} %param.7) | copy-start | bytes 6148
  152.9 309.7 %all-to-all-start = ((bf16[8,4,800,512]{3,2,1,0:T(8,128)(2,1)}), bf16[8,4,800,512]{3,2,1,0:T(8,128)(2,1)}, u32[]{:S(2)}, u32[]{:S(2)}) async-start(bf16[8,4,800,512]{3,2,1,0:T(8,128)(2,1)} %fusion), calls=%async_computation | async-start | bytes 52428800 | tf_op jit(solution)/shard_map/all_to_all | solution.py:13
Sparse Core Ops, SparseCore 0:
  32.2 54.7 all-reduce.1
